TPU v7x, 32 devices: a whole 2x2x4 slice. The times are simulated.
32 devices in a mesh: row: 8 (over z, y), ma: 4 (over x, core).
Axes of the slice: x: 2, y: 2, z: 4, core: 2. Of those that a mesh axis runs over, the one named last changes fastest.
Arguments:
- thermal_state: float32 [64, 768, 2048], P('row', None, 'ma'), may hold values from -6 to 6
- sphere_node_annulus: int32 [64, 768], P('row'), may hold values from 0 to 1022, as said below
- sphere_node_offset: float32 [64, 768], P('row'), may hold values from 0 to 1
- integration_share: float32 [64, 768], P('row'), may hold values from 0.02 to 0.2
- annulus_holder_row: int32 [1024], replicated, may hold values from 0 to 7, never falling along the last dimension, each value on 1 to 256 neighbouring positions
- rotating_flow_potential: float32 [2048, 2048], P('row', 'ma'), may hold values from -6 to 6
Outputs:
- thermal_state_later: float32 [64, 768, 2048], P('row', None, 'ma')
- flow_potential_later: float32 [2048, 2048], P('row', 'ma')
Inputs may be any that keep to these rules, and one draw needn't show every extreme that they name: `sphere_node_annulus`: lower cell of each point; the next cell exists. `annulus_holder_row`: never falling along cells; each owner holds 1 to 256 cells and some owner exactly 256.
All inputs are finite; a program needn't handle non-finite values.
Results may differ from a plain program's by a relative error of at most 0.0003.
Values sent between devices are 32-bit elements; how exact they have to be, the bound alone decides.
A program may use at most 64 MiB of HBM per device.

v0:
```python
import math
import jax
import jax.numpy as jnp
from jax import lax
from jax.sharding import PartitionSpec as P

stream_step = 0.5
thermal_advance = 0.25


def extended(x, sides, width, wrap):
    for axis, dim in sides:
        size, length = (lax.axis_size(axis), x.shape[dim])
        up = [(i, (i + 1) % size) for i in range(size if wrap else size - 1)]
        down = [(j, i) for i, j in up]
        last = lax.slice_in_dim(x, length - width, length, axis=dim)
        leading = lax.slice_in_dim(x, 0, width, axis=dim)
        before = lax.ppermute(last, axis, up)
        after = lax.ppermute(leading, axis, down)
        x = jnp.concatenate([before, x, after], axis=dim)
    return x


def phi_diff(field):
    return (field[:, 2:] - field[:, :-2]) * 0.5


def qg_step(zint, stream, geo_slots):
    geo_column = geo_slots[:, None]
    extended_field = extended(jnp.stack([zint, stream]), (("ma", 2),), 2, True)
    forcing = -geo_column * phi_diff(extended_field[0])
    stream_wide = extended_field[1][:, 1:-1] + stream_step * forcing
    velocity = geo_column * phi_diff(stream_wide)
    return (stream_wide[:, 1:-1], velocity)


def per_device(
    thermal_state,
    sphere_node_annulus,
    sphere_node_offset,
    integration_share,
    annulus_holder_row,
    rotating_flow_potential,
):
    sphere_level_list, meridian_total, longitude_total = thermal_state.shape
    slot_most = rotating_flow_potential.shape[0]
    cell_count = annulus_holder_row.shape[0]
    cells = jnp.arange(cell_count, dtype=jnp.int32)
    before = jnp.sum(
        (annulus_holder_row[None, :] < annulus_holder_row[:, None]).astype(jnp.int32), axis=1
    )
    slot_of_cell = annulus_holder_row * slot_most + cells - before
    geo_cell = 1.0 / (0.25 + (cells.astype(jnp.float32) + 0.5) / cell_count)
    lower_cell = sphere_node_annulus.reshape(-1)
    slot_low = slot_of_cell[lower_cell]
    slot_high = slot_of_cell[lower_cell + 1]
    fraction = sphere_node_offset.reshape(-1)
    quadrature = integration_share.reshape(-1)
    below_share = quadrature * (1.0 - fraction)
    above_share = quadrature * fraction
    heat_vector_linear = thermal_state.reshape(-1, longitude_total)
    own_index = lax.axis_index("row")
    own_start = own_index * slot_most
    slot_rows = jnp.arange(lax.axis_size("row") * slot_most, dtype=jnp.int32)
    banded = jnp.where(slot_rows[:, None] == slot_low[None, :], below_share[None, :], 0.0)
    banded = banded + jnp.where(slot_rows[:, None] == slot_high[None, :], above_share[None, :], 0.0)
    zint = lax.psum_scatter(
        jnp.dot(
            banded,
            heat_vector_linear,
            precision=lax.Precision.HIGHEST,
            preferred_element_type=jnp.float32,
        ),
        "row",
        scatter_dimension=0,
        tiled=True,
    )
    slot_rows = own_start + jnp.arange(slot_most, dtype=jnp.int32)
    hits = slot_of_cell[None, :] == slot_rows[:, None]
    flow_potential_later, velocity = qg_step(
        zint, rotating_flow_potential, jnp.sum(jnp.where(hits, geo_cell[None, :], 0.0), axis=1)
    )
    piece = lax.all_gather(velocity, "row", axis=0, tiled=True)
    slot_cols = jnp.arange(piece.shape[0], dtype=jnp.int32)
    interp = jnp.where(slot_low[:, None] == slot_cols[None, :], (1.0 - fraction)[:, None], 0.0)
    interp = interp + jnp.where(slot_high[:, None] == slot_cols[None, :], fraction[:, None], 0.0)
    shifted_heat = jnp.dot(
        interp, piece, precision=lax.Precision.HIGHEST, preferred_element_type=jnp.float32
    )
    sphere_node_drift = shifted_heat.reshape(sphere_level_list, meridian_total, longitude_total)
    annulus_edges = extended(thermal_state, (("row", 0),), 1, False)
    distance_from_centre = (annulus_edges[2:] - annulus_edges[:-2]) * 0.5
    wrapped_heat_grid = jnp.pad(thermal_state, ((0, 0), (1, 1), (0, 0)))
    theta_from_north = (wrapped_heat_grid[:, 2:] - wrapped_heat_grid[:, :-2]) * 0.5
    angle = math.pi * (jnp.arange(meridian_total, dtype=jnp.float32) + 0.5) / meridian_total
    sin_theta_term = jnp.sin(angle)[None, :, None]
    cos_theta_term = jnp.cos(angle)[None, :, None]
    thermal_state_later = thermal_state - thermal_advance * sphere_node_drift * (
        sin_theta_term * distance_from_centre + cos_theta_term * theta_from_north
    )
    return (thermal_state_later, flow_potential_later)


def solution(mesh):
    return jax.shard_map(
        per_device,
        mesh=mesh,
        in_specs=(
            P("row", None, "ma"),
            P("row", None),
            P("row", None),
            P("row", None),
            P(),
            P("row", "ma"),
        ),
        out_specs=(P("row", None, "ma"), P("row", "ma")),
        check_vma=False,
    )
```

profile of v0, /device:TPU:0, one launch (start us, length us, event | category | flops | bytes accessed | tf_op | source)
XLA Modules:
  0.0 537.9 jit_solution(14528305836900812789)
XLA Ops:
  7.2 0.0 reduce-scatter.2.cloned.1.call-start
  7.2 1.3 convert_reduce_fusion
  8.5 0.7 add_subtract_fusion
  9.2 0.7 reshape.131
  10.0 0.8 copy.8
  10.7 0.7 reshape.132
  11.5 0.1 compare_select_fusion.1
  11.6 24.8 %gather_fusion = s32[6144]{0:T(1024)S(1)} fusion(s32[1024]{0:T(1024)S(1)} %add_subtract_fusion, s32[6144]{0:T(1024)S(1)} %broadcast_clamp_fusion.1), kind=kCustom, calls=%fused_computation | custom fusion | bytes 73728 | tf_op jit(solution)/shard_map/gather | solution.py:55
  36.3 24.8 %gather_fusion.1 = s32[6144]{0:T(1024)S(1)} fusion(s32[1024]{0:T(1024)S(1)} %add_subtract_fusion, s32[6144]{0:T(1024)S(1)} %broadcast_clamp_fusion), kind=kCustom, calls=%fused_computation.1 | custom fusion | bytes 73728 | tf_op jit(solution)/shard_map/gather | solution.py:56
  61.1 0.0 copy-start
  61.2 93.2 %fusion = f32[2048,512]{1,0:T(8,128)} fusion(f32[6144,512]{1,0:T(8,128)} %bitcast.18, f32[6144]{0:T(1024)S(1)} %get-tuple-element.11, s32[6144]{0:T(1024)S(1)} %gather_fusion.1, f32[6144]{0:T(1024)S(1)} %get-tuple-element.10, s32[6144]{0:T(1024)S(1)} %gather_fusion), kind=kOutput, calls=%fused_computation.2 | convolution fusion | flops 77372325888 | bytes 16875520 | tf_op jit(solution)/shard_map/dot_general | solution.py:68
  154.3 0.0 reduce-scatter.2.cloned.1.call-update
  154.4 0.0 all-gather.2.cloned.1.call-start
  154.4 0.2 select_reduce_fusion
  154.7 90.8 %reduce-scatter.2.cloned.1.call-done = f32[256,512]{1,0:T(8,128)} async-done(((f32[2048,512]{1,0:T(8,128)}), f32[256,512]{1,0:T(8,128)}) %reduce-scatter.2.cloned.1.call-update) | async-done | bytes 524304 | tf_op jit(solution)/shard_map/reduce_scatter | solution.py:67
  245.5 0.0 copy-done
  245.5 1.1 pad_maximum_fusion.4
  246.6 0.1 collective-permute-start
  246.7 1.7 collective-permute-start.1
  248.4 5.1 collective-permute-done
  253.5 0.8 collective-permute-done.1
  254.3 1.5 pad_maximum_fusion.2
  255.8 0.1 slice_bitcast_fusion.1
  255.9 0.5 fusion.28
  256.4 1.3 fusion.34
  257.7 0.0 all-gather.2.cloned.1.call-update
  257.7 3.8 fusion.33
  261.6 1.3 collective-permute-start.2
  262.9 4.6 collective-permute-start.3
  267.6 110.0 %all-gather.2.cloned.1.call-done = f32[2048,512]{1,0:T(8,128)} async-done(((f32[256,512]{1,0:T(8,128)}), f32[2048,512]{1,0:T(8,128)}) %all-gather.2.cloned.1.call-update) | async-done | bytes 4194320 | tf_op jit(solution)/shard_map/all_gather | solution.py:83
  377.6 123.0 %fusion.23 = f32[6144,512]{1,0:T(8,128)} fusion(f32[2048,512]{1,0:T(8,128)} %all-gather.2.cloned.1.call-done, f32[6144]{0:T(1024)S(1)} %reshape.131, s32[6144]{0:T(1024)S(1)} %gather_fusion.1, f32[6144]{0:T(1024)S(1)} %get-tuple-element.12, s32[6144]{0:T(1024)S(1)} %gather_fusion), kind=kOutput, calls=%fused_computation.31 | convolution fusion | flops 77375471616 | bytes 16875520 | tf_op jit(solution)/shard_map/dot_general | solution.py:87
  500.6 0.0 collective-permute-done.2
  500.6 0.0 collective-permute-done.3
  500.6 30.5 %fusion.22 = f32[8,768,512]{2,1,0:T(8,128)} fusion(f32[8,768,512]{2,1,0:T(8,128)} %param.6, f32[8,768,512]{2,1,0:T(8,128)} %bitcast.19, f32[1,768,512]{2,1,0:T(8,128)S(1)} %collective-permute-done.3, f32[1,768,512]{2,1,0:T(8,128)S(1)} %collective-permute-done.2, f32[768]{0:T(1024)S(1)} %get-tuple-element.17, f32[768]{0:T(1024)S(1)} %get-tuple-element.18), kind=kLoop, calls=%fused_computation.29 | loop fusion | flops 28311552 | bytes 40900608 | tf_op jit(solution)/shard_map/sub | solution.py:98
  (7 shorter events, 0.1 us)
Async XLA Ops:
  7.2 238.4 %reduce-scatter.2.cloned.1.call-start = ((), (), s32[]{:S(2)}) async-start(), calls=%async_computation.1 | async-start | bytes 4718592 | tf_op jit(solution)/shard_map/reduce_scatter | solution.py:67
  61.1 184.4 %copy-start = (f32[256,512]{1,0:T(8,128)S(1)}, f32[256,512]{1,0:T(8,128)}, u32[]{:S(2)}) copy-start(f32[256,512]{1,0:T(8,128)} %param.11) | copy-start | bytes 1572868
  154.4 223.2 %all-gather.2.cloned.1.call-start = ((), (), s32[]{:S(2)}) async-start(), calls=%async_computation.2 | async-start | bytes 4718592 | tf_op jit(solution)/shard_map/all_gather | solution.py:83
  246.6 6.9 %collective-permute-start = (f32[2,256,2]{2,1,0:T(8,128)S(1)}, f32[2,256,2]{2,1,0:T(8,128)S(1)}, u32[]{:S(2)}, u32[]{:S(2)}) collective-permute-start(f32[2,256,2]{2,1,0:T(8,128)S(1)} %get-tuple-element.6), channel_id=1, source_target_pairs={{0,1},{1,2},{2,3},{3,0},{4,5},{5,6},{6,7},{7,4},{8,9},{9,10},{10,1... | collective-permute-start | bytes 12296 | tf_op jit(solution)/shard_map/ppermute | solution.py:18
  246.7 7.6 %collective-permute-start.1 = (f32[2,256,2]{2,1,0:T(8,128)S(1)}, f32[2,256,2]{2,1,0:T(8,128)S(1)}, u32[]{:S(2)}, u32[]{:S(2)}) collective-permute-start(f32[2,256,2]{2,1,0:T(8,128)S(1)} %get-tuple-element.7), channel_id=1, source_target_pairs={{1,0},{2,1},{3,2},{0,3},{5,4},{6,5},{7,6},{4,7},{9,8},{10,9},{11,1... | collective-permute-start | bytes 12296 | tf_op jit(solution)/shard_map/ppermute | solution.py:19
  261.6 239.0 %collective-permute-start.2 = (f32[1,768,512]{2,1,0:T(8,128)}, f32[1,768,512]{2,1,0:T(8,128)S(1)}, u32[]{:S(2)}, u32[]{:S(2)}) collective-permute-start(f32[1,768,512]{2,1,0:T(8,128)} %get-tuple-element.2), channel_id=1, source_target_pairs={{4,0},{8,4},{12,8},{16,12},{20,16},{24,20},{28,24},{5,1},{9,5},{13... | collective-permute-start | bytes 4718600 | tf_op jit(solution)/shard_map/ppermute | solution.py:19
  262.9 237.7 %collective-permute-start.3 = (f32[1,768,512]{2,1,0:T(8,128)}, f32[1,768,512]{2,1,0:T(8,128)S(1)}, u32[]{:S(2)}, u32[]{:S(2)}) collective-permute-start(f32[1,768,512]{2,1,0:T(8,128)} %get-tuple-element.3), channel_id=1, source_target_pairs={{0,4},{4,8},{8,12},{12,16},{16,20},{20,24},{24,28},{1,5},{5,9},{9,... | collective-permute-start | bytes 4718600 | tf_op jit(solution)/shard_map/ppermute | solution.py:18
Sparse Core Ops, SparseCore 0:
  154.5 90.9 reduce-scatter.1
  257.9 119.6 all-gather.1
where the time goes:
time: 538 us
  matrix products  216 us (40%)
  waiting for transfers between devices  207 us (38%)
  local copies, waits for them, and re-layouts  55.7 us (10%)
  other arithmetic  37.3 us (7%)
  between operations  14.2 us (3%)
  starting transfers between devices  7.8 us (1%)
    dot_general x1, matrix products, per_device(): jnp.dot(interp, piece, precision=lax.Precision.HIGHEST, preferred_element...  123 us
    all_gather x1, waiting for transfers between devices, per_device(): piece = lax.all_gather(velocity, 'row', axis=0, tiled=True)  110 us
    dot_general x1, matrix products, per_device(): jnp.dot(banded, heat_vector_linear, precision=lax.Precision.HIGHEST, pref...  93.2 us
    reduce_scatter x1, waiting for transfers between devices, per_device(): lax.psum_scatter(jnp.dot(banded, heat_vector_linear, precision=lax.Precis...  90.8 us
    sub x1, other arithmetic, per_device(): thermal_state - thermal_advance * sphere_node_drift * (sin_theta_term * d...  30.5 us
    gather x1, local copies, waits for them, and re-layouts, per_device(): slot_low = slot_of_cell[lower_cell]  24.8 us
    gather x1, local copies, waits for them, and re-layouts, per_device(): slot_high = slot_of_cell[lower_cell + 1]  24.8 us
  transfers between devices with their start and end apart: 6, of which 4 were waited for; matrix products, arithmetic and copies ran while one was open for 24% of the time, Pallas kernels for 0%

commit v1 on v0

--- a/solution.py
+++ b/solution.py
@@ -80,7 +80,9 @@
     flow_potential_later, velocity = qg_step(
         zint, rotating_flow_potential, jnp.sum(jnp.where(hits, geo_cell[None, :], 0.0), axis=1)
     )
-    piece = lax.all_gather(velocity, "row", axis=0, tiled=True)
+    piece = jnp.concatenate(
+        lax.all_to_all(jnp.stack([velocity] * lax.axis_size("row")), "row", 0, 0), axis=0
+    )
     slot_cols = jnp.arange(piece.shape[0], dtype=jnp.int32)
     interp = jnp.where(slot_low[:, None] == slot_cols[None, :], (1.0 - fraction)[:, None], 0.0)
     interp = interp + jnp.where(slot_high[:, None] == slot_cols[None, :], fraction[:, None], 0.0)

time: 538 us -> 514 us (0.955)
  the two profiles are of different devices: /device:TPU:0 before, /device:TPU:13 now
where the time goes in v1:
time: 514 us
  waiting for transfers between devices  214 us (42%)
  matrix products  209 us (41%)
  local copies, waits for them, and re-layouts  56.6 us (11%)
  between operations  14.2 us (3%)
  starting transfers between devices  12.9 us (3%)
  other arithmetic  6.62 us (1%)
    ppermute x2, waiting for transfers between devices, extended(): after = lax.ppermute(leading, axis, down)  119 us
    dot_general x1, matrix products, per_device(): jnp.dot(interp, piece, precision=lax.Precision.HIGHEST, preferred_element...  116 us
    dot_general x1, matrix products, per_device(): jnp.dot(banded, heat_vector_linear, precision=lax.Precision.HIGHEST, pref...  93.2 us
    reduce_scatter x1, waiting for transfers between devices, per_device(): lax.psum_scatter(jnp.dot(banded, heat_vector_linear, precision=lax.Precis...  89.1 us
    gather x1, local copies, waits for them, and re-layouts, per_device(): slot_low = slot_of_cell[lower_cell]  24.8 us
    gather x1, local copies, waits for them, and re-layouts, per_device(): slot_high = slot_of_cell[lower_cell + 1]  24.8 us
  transfers between devices with their start and end apart: 6, of which 4 were waited for; matrix products, arithmetic and copies ran while one was open for 0% of the time, Pallas kernels for 0%

profile of v1, /device:TPU:13, one launch (start us, length us, event | category | flops | bytes accessed | tf_op | source)
XLA Modules:
  0.0 513.5 jit_solution(8957935394605597259)
XLA Ops:
  7.2 0.0 reduce-scatter.2.cloned.1.call-start
  7.2 1.3 convert_reduce_fusion
  8.5 0.7 add_subtract_fusion
  9.2 0.8 copy.8
  10.0 0.7 reshape.193
  10.7 0.7 reshape.194
  11.5 0.1 compare_select_fusion.1
  11.6 24.8 %gather_fusion = s32[6144]{0:T(1024)S(1)} fusion(s32[1024]{0:T(1024)S(1)} %add_subtract_fusion, s32[6144]{0:T(1024)S(1)} %broadcast_clamp_fusion.1), kind=kCustom, calls=%fused_computation | custom fusion | bytes 73728 | tf_op jit(solution)/shard_map/gather | solution.py:55
  36.3 24.8 %gather_fusion.1 = s32[6144]{0:T(1024)S(1)} fusion(s32[1024]{0:T(1024)S(1)} %add_subtract_fusion, s32[6144]{0:T(1024)S(1)} %broadcast_clamp_fusion), kind=kCustom, calls=%fused_computation.1 | custom fusion | bytes 73728 | tf_op jit(solution)/shard_map/gather | solution.py:56
  61.1 0.0 copy-start
  61.2 93.2 %fusion.2 = f32[2048,512]{1,0:T(8,128)} fusion(f32[6144,512]{1,0:T(8,128)} %bitcast.31, f32[6144]{0:T(1024)S(1)} %get-tuple-element.11, s32[6144]{0:T(1024)S(1)} %gather_fusion.1, f32[6144]{0:T(1024)S(1)} %get-tuple-element.10, s32[6144]{0:T(1024)S(1)} %gather_fusion), kind=kOutput, calls=%fused_computation.4 | convolution fusion | flops 77372325888 | bytes 16875520 | tf_op jit(solution)/shard_map/dot_general | solution.py:68
  154.3 0.0 reduce-scatter.2.cloned.1.call-update
  154.4 0.2 select_reduce_fusion
  154.6 89.1 %reduce-scatter.2.cloned.1.call-done = f32[256,512]{1,0:T(8,128)} async-done(((f32[2048,512]{1,0:T(8,128)}), f32[256,512]{1,0:T(8,128)}) %reduce-scatter.2.cloned.1.call-update) | async-done | bytes 524304 | tf_op jit(solution)/shard_map/reduce_scatter | solution.py:67
  243.7 0.0 copy-done
  243.7 1.1 pad_maximum_fusion.4
  244.9 2.2 collective-permute-start
  247.1 0.0 collective-permute-start.1
  247.1 5.3 %collective-permute-done = f32[2,256,2]{2,1,0:T(8,128)S(1)} collective-permute-done((f32[2,256,2]{2,1,0:T(8,128)S(1)}, f32[2,256,2]{2,1,0:T(8,128)S(1)}, u32[]{:S(2)}, u32[]{:S(2)}) %collective-permute-start) | collective-permute-done | bytes 4128 | tf_op jit(solution)/shard_map/ppermute | solution.py:18
  252.3 1.6 collective-permute-done.1
  253.9 1.5 pad_maximum_fusion.2
  255.4 0.1 slice_bitcast_fusion.1
  255.5 0.0 copy-start.1
  255.5 0.4 fusion.28
  256.0 1.2 fusion.33
  257.2 2.5 stack.11
  259.7 4.5 all-to-all-start
  264.2 2.2 fusion.32
  266.4 2.2 collective-permute-start.2
  268.6 4.0 collective-permute-start.3
  272.7 0.0 copy-done.1
  272.7 117.9 %collective-permute-done.2 = f32[1,768,512]{2,1,0:T(8,128)} collective-permute-done((f32[1,768,512]{2,1,0:T(8,128)S(1)}, f32[1,768,512]{2,1,0:T(8,128)}, u32[]{:S(2)}, u32[]{:S(2)}) %collective-permute-start.2) | collective-permute-done | bytes 1572896 | tf_op jit(solution)/shard_map/ppermute | solution.py:19
  390.6 0.0 collective-permute-done.3
  390.6 0.0 all-to-all-done
  390.6 116.0 %fusion.23 = f32[8,768,512]{2,1,0:T(8,128)} fusion(f32[8,768,512]{2,1,0:T(8,128)} %param.6, f32[1,768,512]{2,1,0:T(8,128)} %collective-permute-done.3, f32[1,768,512]{2,1,0:T(8,128)} %collective-permute-done.2, f32[768]{0:T(1024)S(1)} %get-tuple-element.16, f32[768]{0:T(1024)S(1)} %get-tuple-element.17, f32[2048,512,1]{1,0,2:T(8,128)} %bitcast.9, ...), kind=kOutput, calls=%fused_computation.30 | convolution fusion | flops 77403783168 | bytes 32610304 | tf_op jit(solution)/shard_map/dot_general | solution.py:89
  (10 shorter events, 0.1 us)
Async XLA Ops:
  7.2 236.6 %reduce-scatter.2.cloned.1.call-start = ((), (), s32[]{:S(2)}) async-start(), calls=%async_computation.2 | async-start | bytes 4718592 | tf_op jit(solution)/shard_map/reduce_scatter | solution.py:67
  61.1 182.6 %copy-start = (f32[256,512]{1,0:T(8,128)S(1)}, f32[256,512]{1,0:T(8,128)}, u32[]{:S(2)}) copy-start(f32[256,512]{1,0:T(8,128)} %param.11) | copy-start | bytes 1572868
  244.9 7.5 %collective-permute-start = (f32[2,256,2]{2,1,0:T(8,128)S(1)}, f32[2,256,2]{2,1,0:T(8,128)S(1)}, u32[]{:S(2)}, u32[]{:S(2)}) collective-permute-start(f32[2,256,2]{2,1,0:T(8,128)S(1)} %get-tuple-element.6), channel_id=1, source_target_pairs={{0,1},{1,2},{2,3},{3,0},{4,5},{5,6},{6,7},{7,4},{8,9},{9,10},{10,1... | collective-permute-start | bytes 12296 | tf_op jit(solution)/shard_map/ppermute | solution.py:18
  247.1 6.8 %collective-permute-start.1 = (f32[2,256,2]{2,1,0:T(8,128)S(1)}, f32[2,256,2]{2,1,0:T(8,128)S(1)}, u32[]{:S(2)}, u32[]{:S(2)}) collective-permute-start(f32[2,256,2]{2,1,0:T(8,128)S(1)} %get-tuple-element.7), channel_id=1, source_target_pairs={{1,0},{2,1},{3,2},{0,3},{5,4},{6,5},{7,6},{4,7},{9,8},{10,9},{11,1... | collective-permute-start | bytes 12296 | tf_op jit(solution)/shard_map/ppermute | solution.py:19
  255.5 17.2 %copy-start.1 = (f32[8,768]{1,0:T(8,128)S(1)}, f32[8,768]{1,0:T(8,128)}, u32[]{:S(2)}) copy-start(f32[8,768]{1,0:T(8,128)} %param.8) | copy-start | bytes 73732
  259.7 130.9 %all-to-all-start = ((f32[8,256,512]{2,1,0:T(8,128)}), f32[8,256,512]{2,1,0:T(8,128)}, u32[]{:S(2)}, u32[]{:S(2)}) async-start(f32[8,256,512]{2,1,0:T(8,128)} %stack.11), calls=%async_computation.1 | async-start | bytes 8388608 | tf_op jit(solution)/shard_map/all_to_all | solution.py:84
  266.4 124.2 %collective-permute-start.2 = (f32[1,768,512]{2,1,0:T(8,128)S(1)}, f32[1,768,512]{2,1,0:T(8,128)}, u32[]{:S(2)}, u32[]{:S(2)}) collective-permute-start(f32[1,768,512]{2,1,0:T(8,128)S(1)} %get-tuple-element.2), channel_id=1, source_target_pairs={{4,0},{8,4},{12,8},{16,12},{20,16},{24,20},{28,24},{5,1},{9,5},{13... | collective-permute-start | bytes 4718600 | tf_op jit(solution)/shard_map/ppermute | solution.py:19
  268.6 122.0 %collective-permute-start.3 = (f32[1,768,512]{2,1,0:T(8,128)S(1)}, f32[1,768,512]{2,1,0:T(8,128)}, u32[]{:S(2)}, u32[]{:S(2)}) collective-permute-start(f32[1,768,512]{2,1,0:T(8,128)S(1)} %get-tuple-element.3), channel_id=1, source_target_pairs={{0,4},{4,8},{8,12},{12,16},{16,20},{20,24},{24,28},{1,5},{5,9},{9,... | collective-permute-start | bytes 4718600 | tf_op jit(solution)/shard_map/ppermute | solution.py:18
Sparse Core Ops, SparseCore 0:
  154.5 89.2 reduce-scatter.1
